TPU v7x, 32 devices: a whole 2x2x4 slice. The times are simulated.
32 devices in a mesh: gx: 4 (over z), gy: 2 (over core), gz: 4 (over y, x).
Axes of the slice: x: 2, y: 2, z: 4, core: 2. Of those that a mesh axis runs over, the one named last changes fastest.
Arguments:
- pair: bfloat16 [128, 512, 512], P('gz', 'gx', 'gy'), may hold values from -6 to 6
- pair_mask: int32 [512, 512], P('gx', 'gy'), may hold values from 0 to 1, as said below
- input_gain: float32 [128], replicated, may hold values from 0.1 to 1.9
- input_weights: bfloat16 [4, 128, 128], replicated, may hold values from -0.5 to 0.5
- out_gate_weight: bfloat16 [128, 128], replicated, may hold values from -0.5 to 0.5
- hidden_gain: float32 [128], replicated, may hold values from 0.1 to 1.9
- out_weight: bfloat16 [128, 128], replicated, may hold values from -0.5 to 0.5
Outputs:
- update: bfloat16 [128, 512, 512], P('gz', 'gx', 'gy')
Inputs may be any that keep to these rules, and one draw needn't show every extreme that they name: pair_mask[r, s] = m[r] * m[s] for a 0/1 residue mask m of the draw that is 0 for all r >= L, for one crop length L with 256 < L <= 512; residues below L may also be 0.
All inputs are finite; a program needn't handle non-finite values.
Results may differ from a plain program's by a relative error of at most 0.011.
Values may be sent and summed in bfloat16 or wider, within the bound.
No kernel may reach another device: no remote copies, remote signals or barrier semaphores. Data moves between devices by JAX's collectives and lax.ppermute only.
A program may use at most 64 MiB of HBM per device.

v0:
```python
import jax
import jax.numpy as jnp
from jax import lax
from jax.sharding import PartitionSpec as P

EPSILON = 1e-05


def own_columns(matrix, width):
    first = lax.axis_index("gz") * width
    return lax.dynamic_slice_in_dim(matrix, first, width, matrix.ndim - 1)


def gated_sides(weights, normed, mask_values, hidden):
    joined = jnp.concatenate([weights[0], weights[1]], axis=1)
    product = jnp.einsum("dk,drs->krs", joined, normed, preferred_element_type=jnp.float32)
    return (mask_values * jax.nn.sigmoid(product[:hidden]) * product[hidden:]).astype(jnp.bfloat16)


def shards(pair, pair_mask, input_gain, input_weights, out_gate_weight, hidden_gain, out_weight):
    local_channels = pair.shape[0]
    all_channels = input_gain.shape[0]
    all_hidden = hidden_gain.shape[0]
    local_hidden = all_hidden // lax.axis_size("gz")
    mask_values = pair_mask.astype(jnp.float32)
    values = pair.astype(jnp.float32)
    moments = lax.psum((jnp.sum(values, axis=0), jnp.sum(values * values, axis=0)), "gz")
    average = moments[0] / all_channels
    spread = moments[1] / all_channels - average * average
    gains = own_columns(input_gain, local_channels)
    normed_local = ((values - average) * lax.rsqrt(spread + EPSILON) * gains[:, None, None]).astype(
        jnp.bfloat16
    )
    normed = lax.all_gather(normed_local, "gz", axis=0, tiled=True)
    side_weights = own_columns(input_weights, local_hidden)
    left_side = gated_sides(side_weights[0:2], normed, mask_values, local_hidden)
    right_side = gated_sides(side_weights[2:4], normed, mask_values, local_hidden)
    gate_weights = own_columns(out_gate_weight, local_channels)
    gate = jax.nn.sigmoid(
        jnp.einsum("dc,drs->crs", gate_weights, normed, preferred_element_type=jnp.float32)
    )
    left_panels = lax.all_gather(left_side, "gy", axis=2, tiled=True)
    row_blocks = lax.all_to_all(left_panels, "gx", split_axis=2, concat_axis=1, tiled=True)
    triangle = jnp.einsum(
        "cki,ckj->icj",
        row_blocks,
        lax.all_gather(right_side, "gx", axis=1, tiled=True),
        preferred_element_type=jnp.float32,
    )
    hidden_gains = own_columns(hidden_gain, local_hidden)
    hidden_stats = lax.psum((jnp.sum(triangle, axis=1), jnp.sum(triangle * triangle, axis=1)), "gz")
    hidden_mean = hidden_stats[0] / all_hidden
    hidden_spread = hidden_stats[1] / all_hidden - hidden_mean * hidden_mean
    hidden_normed = (
        (triangle - hidden_mean[:, None, :])
        * lax.rsqrt(hidden_spread + EPSILON)[:, None, :]
        * hidden_gains[None, :, None]
    ).astype(jnp.bfloat16)
    every_hidden = lax.all_gather(hidden_normed, "gz", axis=1, tiled=True)
    out_columns = own_columns(out_weight, local_channels)
    projected = jnp.einsum(
        "hc,ihj->cij", out_columns, every_hidden, preferred_element_type=jnp.float32
    )
    return (mask_values * gate * projected).astype(jnp.bfloat16)


def solution(mesh):
    placed = (P("gz", "gx", "gy"), P("gx", "gy"), P(), P(), P(), P(), P())
    return jax.shard_map(
        shards, mesh=mesh, in_specs=placed, out_specs=P("gz", "gx", "gy"), check_vma=False
    )
```

profile of v0, /device:TPU:0, one launch (start us, length us, event | category | flops | bytes accessed | tf_op | source)
XLA Modules:
  0.0 593.2 jit_solution(12267018574907195706)
XLA Ops:
  6.5 0.0 copy-start
  6.5 0.0 copy-start.1
  6.5 0.0 all-reduce.7.cloned.1.call-start
  6.5 4.8 convert_reduce_fusion
  11.3 0.0 copy-start.2
  11.3 0.0 copy-start.3
  11.3 0.0 all-reduce.7.cloned.1.call-update
  11.3 0.0 all-gather.5.cloned.1.call-start
  11.4 0.8 dynamic_slice.16
  12.2 45.1 %all-reduce.7.cloned.1.call-done = (f32[128,256]{1,0:T(8,128)}, f32[128,256]{1,0:T(8,128)}) async-done(((f32[128,256]{1,0:T(8,128)}, f32[128,256]{1,0:T(8,128)}), (f32[128,256]{1,0:T(8,128)}, f32[128,256]{1,0:T(8,128)})) %all-reduce.7.cloned.1.call-update) | async-done | bytes 262160 | tf_op jit(solution)/shard_map/psum | solution.py:27
  57.3 1.0 broadcast_multiply_fusion.1
  58.3 0.0 copy-done.1
  58.3 3.0 fusion.6
  61.4 0.0 all-gather.5.cloned.1.call-update
  61.4 0.0 all-gather.9.cloned.1.call-start
  61.4 0.0 copy-done.2
  61.4 0.1 constant_dynamic-slice_fusion.2
  61.6 0.1 copy.49
  61.6 0.1 copy.50
  61.7 0.1 copy.47
  61.8 0.1 copy.48
  61.9 0.0 copy-done.3
  61.9 87.1 %all-gather.5.cloned.1.call-done = bf16[128,128,256]{2,0,1:T(8,128)(2,1)} async-done(((bf16[32,128,256]{2,0,1:T(8,128)(2,1)}), bf16[128,128,256]{2,0,1:T(8,128)(2,1)}) %all-gather.5.cloned.1.call-update) | async-done | bytes 8388624 | tf_op jit(solution)/shard_map/all_gather | solution.py:34
  149.0 0.0 slice-start
  149.0 0.0 slice-start.1
  149.0 4.8 fusion.29
  153.8 0.0 slice-done
  153.8 1.0 slice-done.1
  154.9 1.3 fusion.26
  156.2 4.1 fusion.13
  160.2 0.0 all-gather.9.cloned.1.call-update
  160.2 0.0 all-gather.7.cloned.1.call-start
  160.3 0.5 all-gather.7.cloned.1.call-update
  160.8 0.0 all-reduce.5.cloned.1.call-start
  160.9 12.3 %all-gather.9.cloned.1.call-done = bf16[32,128,512]{2,0,1:T(8,128)(2,1)} async-done(((bf16[32,128,256]{2,0,1:T(8,128)(2,1)}), bf16[32,128,512]{2,0,1:T(8,128)(2,1)}) %all-gather.9.cloned.1.call-update) | async-done | bytes 4194320 | tf_op jit(solution)/shard_map/all_gather | solution.py:42
  173.2 9.2 %copy.34 = bf16[32,128,512]{1,0,2:T(8,128)(2,1)} copy(bf16[32,128,512]{2,0,1:T(8,128)(2,1)} %all-gather.9.cloned.1.call-done) | data formatting | bytes 8388608 | tf_op jit(solution)/shard_map/all_gather | solution.py:42
  182.3 210.0 %all_to_all.18 = bf16[32,128,512]{1,0,2:T(8,128)(2,1)} all-to-all(bf16[32,128,512]{1,0,2:T(8,128)(2,1)} %copy.34), channel_id=1, replica_groups=mesh['gx'=4,'gy'=2,'gz'=4] {'gx'}, dimensions={2} | all-to-all | bytes 8388608 | tf_op jit(solution)/shard_map/all_to_all | solution.py:43
  392.4 7.6 %copy.35 = bf16[32,128,4,128]{3,1,2,0:T(8,128)(2,1)} copy(bf16[32,128,4,128]{1,0,3,2:T(8,128)(2,1)} %bitcast.40) | data formatting | bytes 8388608 | tf_op jit(solution)/shard_map/all_to_all | solution.py:43
  399.9 14.9 %all-gather.7.cloned.1.call-done = bf16[32,512,256]{2,0,1:T(8,128)(2,1)} async-done(((bf16[32,128,256]{2,0,1:T(8,128)(2,1)}), bf16[32,512,256]{2,0,1:T(8,128)(2,1)}) %all-gather.7.cloned.1.call-update) | async-done | bytes 8388624 | tf_op jit(solution)/shard_map/all_gather | solution.py:47
  414.9 0.0 copy-start.5
  414.9 17.5 %bitcast_reduce_fusion = (f32[128,256]{0,1:T(8,128)S(1)}, f32[128,256]{0,1:T(8,128)S(1)}, f32[32,256,128]{2,1,0:T(8,128)}) fusion(bf16[32,512,128]{2,1,0:T(8,128)(2,1)} %bitcast.41, bf16[32,512,256]{2,0,1:T(8,128)(2,1)} %all-gather.7.cloned.1.call-done), kind=kOutput, calls=%fused_computation.27 | convolution fusion | flops 1076822016 | bytes 17039360 | tf_op jit(solution)/shard_map/cki,ckj->icj/dot_general | solution.py:44
  432.4 0.8 copy.37
  433.2 0.8 copy.39
  433.9 0.0 all-reduce.5.cloned.1.call-update
  433.9 0.3 all-gather.11.cloned.1.call-start
  434.2 0.0 copy-done.5
  434.2 0.1 dynamic_slice.19
  434.3 41.0 %all-reduce.5.cloned.1.call-done = (f32[128,256]{1,0:T(8,128)}, f32[128,256]{1,0:T(8,128)}) async-done(((f32[128,256]{1,0:T(8,128)}, f32[128,256]{1,0:T(8,128)}), (f32[128,256]{1,0:T(8,128)}, f32[128,256]{1,0:T(8,128)})) %all-reduce.5.cloned.1.call-update) | async-done | bytes 262160 | tf_op jit(solution)/shard_map/psum | solution.py:51
  475.3 1.0 broadcast_multiply_fusion
  476.3 0.1 copy.38
  476.4 0.1 copy.40
  476.5 2.9 fusion.20
  479.4 2.9 copy.41
  482.3 0.0 all-gather.11.cloned.1.call-update
  482.3 0.0 copy-start.4
  482.4 87.6 %all-gather.11.cloned.1.call-done = bf16[128,128,256]{2,0,1:T(8,128)(2,1)} async-done(((bf16[128,32,256]{2,0,1:T(8,128)(2,1)}), bf16[128,128,256]{2,0,1:T(8,128)(2,1)}) %all-gather.11.cloned.1.call-update) | async-done | bytes 8388624 | tf_op jit(solution)/shard_map/all_gather | solution.py:59
  570.0 0.0 copy-done
  570.0 8.7 %fusion = f32[32,128,256]{2,0,1:T(8,128)S(1)} fusion(bf16[128,128,256]{2,0,1:T(8,128)(2,1)} %all-gather.11.cloned.1.call-done, bf16[128,128]{1,0:T(8,128)(2,1)S(1)} %copy-done, s32[]{:T(128)S(6)} %select_n.2), kind=kOutput, calls=%fused_computation | convolution fusion | flops 268435456 | bytes 12615684 | tf_op jit(solution)/shard_map/hc,ihj->cij/dot_general | solution.py:61
  578.7 0.0 copy-done.4
  578.7 5.1 multiply_convert_fusion
  583.8 2.5 copy.43
  (2 shorter events, 0.0 us)
Async XLA Ops:
  6.5 563.4 %copy-start = (bf16[128,128]{1,0:T(8,128)(2,1)S(1)}, bf16[128,128]{1,0:T(8,128)(2,1)}, u32[]{:S(2)}) copy-start(bf16[128,128]{1,0:T(8,128)(2,1)} %param.13) | copy-start | bytes 98308
  6.5 51.8 %copy-start.1 = (bf16[32,128,256]{2,1,0:T(8,128)(2,1)S(1)}, bf16[32,128,256]{2,1,0:T(8,128)(2,1)}, u32[]{:S(2)}) copy-start(bf16[32,128,256]{2,1,0:T(8,128)(2,1)} %param.7) | copy-start | bytes 6291460
  6.5 50.8 %all-reduce.7.cloned.1.call-start = ((), (), s32[]{:S(2)}) async-start(), calls=%async_computation.6 | async-start | bytes 524288 | tf_op jit(solution)/shard_map/psum | solution.py:27
  11.3 50.1 %copy-start.2 = (bf16[4,128,128]{2,1,0:T(8,128)(2,1)S(1)}, bf16[4,128,128]{2,1,0:T(8,128)(2,1)}, u32[]{:S(2)}) copy-start(bf16[4,128,128]{2,1,0:T(8,128)(2,1)} %param.10) | copy-start | bytes 393220
  11.3 50.6 %copy-start.3 = (s32[128,256]{1,0:T(8,128)S(1)}, s32[128,256]{1,0:T(8,128)}, u32[]{:S(2)}) copy-start(s32[128,256]{1,0:T(8,128)} %param.8) | copy-start | bytes 393220
  11.3 137.7 %all-gather.5.cloned.1.call-start = ((), (), s32[]{:S(2)}) async-start(), calls=%async_computation.1 | async-start | bytes 10485760 | tf_op jit(solution)/shard_map/all_gather | solution.py:34
  61.4 111.8 %all-gather.9.cloned.1.call-start = ((), (), s32[]{:S(2)}) async-start(), calls=%async_computation.3 | async-start | bytes 6291456 | tf_op jit(solution)/shard_map/all_gather | solution.py:42
  149.0 4.8 slice-start
  149.0 5.9 slice-start.1
  160.2 254.6 %all-gather.7.cloned.1.call-start = ((), (), s32[]{:S(2)}) async-start(), calls=%async_computation.2 | async-start | bytes 10485760 | tf_op jit(solution)/shard_map/all_gather | solution.py:47
  160.8 314.5 %all-reduce.5.cloned.1.call-start = ((), (), s32[]{:S(2)}) async-start(), calls=%async_computation.5 | async-start | bytes 524288 | tf_op jit(solution)/shard_map/psum | solution.py:51
  414.9 19.4 %copy-start.5 = (f32[128]{0:T(128)S(1)}, f32[128]{0:T(128)}, u32[]{:S(2)}) copy-start(f32[128]{0:T(128)} %param.12) | copy-start | bytes 1540
  433.9 136.0 %all-gather.11.cloned.1.call-start = ((), (), s32[]{:S(2)}) async-start(), calls=%async_computation.4 | async-start | bytes 10485760 | tf_op jit(solution)/shard_map/all_gather | solution.py:59
  482.3 96.3 %copy-start.4 = (bf16[128,128]{1,0:T(8,128)(2,1)S(1)}, bf16[128,128]{1,0:T(8,128)(2,1)}, u32[]{:S(2)}) copy-start(bf16[128,128]{1,0:T(8,128)(2,1)} %param.11) | copy-start | bytes 98308
Sparse Core Ops, SparseCore 0:
  11.5 45.8 all-reduce.6
  61.5 87.4 all-gather.4
  160.4 12.7 all-gather.8
  174.6 240.2 all-gather.6
  434.1 41.2 all-reduce.4
  482.5 87.4 all-gather.10
where the time goes:
time: 594 us; the launch traced here: 593 us
  waiting for transfers between devices  289 us (49%)
  blocking collectives  210 us (35%)
  matrix products  37.5 us (6%)
  local copies, waits for them, and re-layouts  26.2 us (4%)
  other arithmetic  16.8 us (3%)
  between operations  13.6 us (2%)
    all_to_all x1, blocking collectives, shards(): lax.all_to_all(left_panels, 'gx', split_axis=2, concat_axis=1, tiled=True)  210 us
    all_gather x1, waiting for transfers between devices, shards(): every_hidden = lax.all_gather(hidden_normed, 'gz', axis=1, tiled=True)  87.6 us
    all_gather x1, waiting for transfers between devices, shards(): normed = lax.all_gather(normed_local, 'gz', axis=0, tiled=True)  87.1 us
    psum x1, waiting for transfers between devices, shards(): lax.psum((jnp.sum(values, axis=0), jnp.sum(values * values, axis=0)), 'gz')  45.1 us
    psum x1, waiting for transfers between devices, shards(): lax.psum((jnp.sum(triangle, axis=1), jnp.sum(triangle * triangle, axis=1)...  41 us
    dot_general x1, matrix products, shards(): jnp.einsum('cki,ckj->icj', row_blocks, lax.all_gather(right_side, 'gx', a...  17.5 us
    all_gather x1, waiting for transfers between devices, shards(): lax.all_gather(right_side, 'gx', axis=1, tiled=True)  14.9 us
    all_gather x1, waiting for transfers between devices, shards(): left_panels = lax.all_gather(left_side, 'gy', axis=2, tiled=True)  12.3 us
  transfers between devices with their start and end apart: 6, of which 6 were waited for; matrix products, arithmetic and copies ran while one was open for 3% of the time, Pallas kernels for 0%

commit v1 on v0

--- a/solution.py
+++ b/solution.py
@@ -31,7 +31,12 @@
     normed_local = ((values - average) * lax.rsqrt(spread + EPSILON) * gains[:, None, None]).astype(
         jnp.bfloat16
     )
-    normed = lax.all_gather(normed_local, "gz", axis=0, tiled=True)
+    ring = [normed_local]
+    for hop in range(3):
+        ring.append(lax.ppermute(ring[-1], "gz", [(dev, (dev + 1) % 4) for dev in range(4)]))
+    normed = jnp.roll(
+        jnp.concatenate(ring[::-1], axis=0), (lax.axis_index("gz") + 1) * ring[0].shape[0], axis=0
+    )
     side_weights = own_columns(input_weights, local_hidden)
     left_side = gated_sides(side_weights[0:2], normed, mask_values, local_hidden)
     right_side = gated_sides(side_weights[2:4], normed, mask_values, local_hidden)

time: 594 us -> 662 us (1.11)
  waiting for transfers between devices: 289 us -> 340 us
  local copies, waits for them, and re-layouts: 26.2 us -> 38.3 us
    ppermute x0 -> x3, waiting for transfers between devices: none -> 139 us  [shards(): lax.ppermute(ring[-1], 'gz', [(dev, (dev + 1) % 4) for dev in range(4)])]
    all_gather x1 -> x0, waiting for transfers between devices: 87.1 us -> none  [shards(): normed = lax.all_gather(normed_local, 'gz', axis=0, tiled=True)]
    unnamed x20 -> x28, local copies, waits for them, and re-layouts: 1.4 us -> 13.6 us
  transfers between devices with their start and end apart: 6 -> 8, of which waited for: 6 -> 8; matrix products, arithmetic and copies ran while one was open for 3% -> 3% of each run, Pallas kernels for 0% -> 0%
where the time goes in v1:
time: 662 us; the launch traced here: 661 us
  waiting for transfers between devices  340 us (51%)
  blocking collectives  210 us (32%)
  local copies, waits for them, and re-layouts  38.3 us (6%)
  matrix products  37.4 us (6%)
  other arithmetic  19 us (3%)
  between operations  13.3 us (2%)
    all_to_all x1, blocking collectives, shards(): lax.all_to_all(left_panels, 'gx', split_axis=2, concat_axis=1, tiled=True)  210 us
    ppermute x3, waiting for transfers between devices, shards(): lax.ppermute(ring[-1], 'gz', [(dev, (dev + 1) % 4) for dev in range(4)])  139 us
    all_gather x1, waiting for transfers between devices, shards(): every_hidden = lax.all_gather(hidden_normed, 'gz', axis=1, tiled=True)  87.6 us
    psum x1, waiting for transfers between devices, shards(): lax.psum((jnp.sum(values, axis=0), jnp.sum(values * values, axis=0)), 'gz')  45.2 us
    psum x1, waiting for transfers between devices, shards(): lax.psum((jnp.sum(triangle, axis=1), jnp.sum(triangle * triangle, axis=1)...  41 us
    dot_general x1, matrix products, shards(): jnp.einsum('cki,ckj->icj', row_blocks, lax.all_gather(right_side, 'gx', a...  17.6 us
    all_gather x1, waiting for transfers between devices, shards(): lax.all_gather(right_side, 'gx', axis=1, tiled=True)  15 us
    unnamed x28, local copies, waits for them, and re-layouts  13.6 us
  transfers between devices with their start and end apart: 8, of which 8 were waited for; matrix products, arithmetic and copies ran while one was open for 3% of the time, Pallas kernels for 0%

profile of v1, /device:TPU:0, one launch (start us, length us, event | category | flops | bytes accessed | tf_op | source)
XLA Modules:
  0.0 660.9 jit_solution(8496221541052185640)
XLA Ops:
  6.5 0.0 copy-start
  6.5 0.0 all-reduce.7.cloned.1.call-start
  6.6 4.8 convert_reduce_fusion
  11.4 0.0 all-reduce.7.cloned.1.call-update
  11.4 0.0 all-gather.6.cloned.1.call-start
  11.4 0.7 dynamic_slice.20
  12.2 45.2 %all-reduce.7.cloned.1.call-done = (f32[128,256]{1,0:T(8,128)}, f32[128,256]{1,0:T(8,128)}) async-done(((f32[128,256]{1,0:T(8,128)}, f32[128,256]{1,0:T(8,128)}), (f32[128,256]{1,0:T(8,128)}, f32[128,256]{1,0:T(8,128)})) %all-reduce.7.cloned.1.call-update) | async-done | bytes 262160 | tf_op jit(solution)/shard_map/psum | solution.py:27
  57.4 1.0 broadcast_multiply_fusion.1
  58.4 0.0 copy-done.1
  58.4 1.7 fusion.12
  60.0 1.5 collective-permute-start
  61.6 46.3 %collective-permute-done = bf16[32,128,256]{2,0,1:T(8,128)(2,1)S(1)} collective-permute-done((bf16[32,128,256]{2,0,1:T(8,128)(2,1)S(1)}, bf16[32,128,256]{2,0,1:T(8,128)(2,1)S(1)}, u32[]{:S(2)}, u32[]{:S(2)}) %collective-permute-start) | collective-permute-done | bytes 2097184 | tf_op jit(solution)/shard_map/ppermute | solution.py:36
  107.9 1.3 copy-done.3
  109.2 0.5 collective-permute-start.1
  109.8 46.5 %collective-permute-done.1 = bf16[32,128,256]{2,0,1:T(8,128)(2,1)} collective-permute-done((bf16[32,128,256]{2,0,1:T(8,128)(2,1)S(1)}, bf16[32,128,256]{2,0,1:T(8,128)(2,1)}, u32[]{:S(2)}, u32[]{:S(2)}) %collective-permute-start.1) | collective-permute-done | bytes 2097184 | tf_op jit(solution)/shard_map/ppermute | solution.py:36
  156.2 0.0 collective-permute-start.2
  156.2 0.1 constant_dynamic-slice_fusion.2
  156.4 0.1 copy.49
  156.4 0.1 copy.50
  156.5 0.1 copy.47
  156.6 0.1 copy.48
  156.8 0.0 copy-start.4
  156.8 45.9 %collective-permute-done.2 = bf16[32,128,256]{2,0,1:T(8,128)(2,1)} collective-permute-done((bf16[32,128,256]{2,0,1:T(8,128)(2,1)}, bf16[32,128,256]{2,0,1:T(8,128)(2,1)}, u32[]{:S(2)}, u32[]{:S(2)}) %collective-permute-start.2) | collective-permute-done | bytes 2097184 | tf_op jit(solution)/shard_map/ppermute | solution.py:36
  202.6 1.8 constant_dynamic-update-slice_fusion.7
  204.4 1.8 constant_dynamic-update-slice_fusion.6
  206.2 0.2 constant_dynamic-update-slice_fusion.5
  206.4 1.6 constant_dynamic-update-slice_fusion.4
  208.1 1.8 constant_dynamic-update-slice_fusion.3
  209.8 1.8 constant_dynamic-update-slice_fusion.2
  211.6 0.2 constant_dynamic-update-slice_fusion.1
  211.8 1.6 constant_dynamic-update-slice_fusion
  213.5 0.0 copy-start.2
  213.5 1.3 fusion.4
  214.8 4.4 copy-done.2
  219.2 4.7 fusion.6
  223.9 4.4 fusion.19
  228.2 0.0 all-gather.6.cloned.1.call-update
  228.3 0.0 all-gather.4.cloned.1.call-start
  228.3 0.7 all-gather.4.cloned.1.call-update
  229.0 0.0 all-reduce.5.cloned.1.call-start
  229.1 12.0 %all-gather.6.cloned.1.call-done = bf16[32,128,512]{2,0,1:T(8,128)(2,1)} async-done(((bf16[32,128,256]{2,0,1:T(8,128)(2,1)}), bf16[32,128,512]{2,0,1:T(8,128)(2,1)}) %all-gather.6.cloned.1.call-update) | async-done | bytes 4194320 | tf_op jit(solution)/shard_map/all_gather | solution.py:47
  241.0 9.1 %copy.34 = bf16[32,128,512]{1,0,2:T(8,128)(2,1)} copy(bf16[32,128,512]{2,0,1:T(8,128)(2,1)} %all-gather.6.cloned.1.call-done) | data formatting | bytes 8388608 | tf_op jit(solution)/shard_map/all_gather | solution.py:47
  250.2 210.2 %all_to_all.18 = bf16[32,128,512]{1,0,2:T(8,128)(2,1)} all-to-all(bf16[32,128,512]{1,0,2:T(8,128)(2,1)} %copy.34), channel_id=1, replica_groups=mesh['gx'=4,'gy'=2,'gz'=4] {'gx'}, dimensions={2} | all-to-all | bytes 8388608 | tf_op jit(solution)/shard_map/all_to_all | solution.py:48
  460.4 7.5 %copy.35 = bf16[32,128,4,128]{3,1,2,0:T(8,128)(2,1)} copy(bf16[32,128,4,128]{1,0,3,2:T(8,128)(2,1)} %bitcast.35) | data formatting | bytes 8388608 | tf_op jit(solution)/shard_map/all_to_all | solution.py:48
  467.9 15.0 %all-gather.4.cloned.1.call-done = bf16[32,512,256]{2,0,1:T(8,128)(2,1)} async-done(((bf16[32,128,256]{2,0,1:T(8,128)(2,1)}), bf16[32,512,256]{2,0,1:T(8,128)(2,1)}) %all-gather.4.cloned.1.call-update) | async-done | bytes 8388624 | tf_op jit(solution)/shard_map/all_gather | solution.py:52
  482.9 17.6 %bitcast_reduce_fusion = (f32[128,256]{0,1:T(8,128)S(1)}, f32[128,256]{0,1:T(8,128)S(1)}, f32[32,256,128]{2,1,0:T(8,128)}) fusion(bf16[32,512,128]{2,1,0:T(8,128)(2,1)} %bitcast.36, bf16[32,512,256]{2,0,1:T(8,128)(2,1)} %all-gather.4.cloned.1.call-done), kind=kOutput, calls=%fused_computation.33 | convolution fusion | flops 1076822016 | bytes 17039360 | tf_op jit(solution)/shard_map/cki,ckj->icj/dot_general | solution.py:49
  500.4 0.7 copy.37
  501.2 0.8 copy.39
  501.9 0.0 all-reduce.5.cloned.1.call-update
  502.0 0.3 all-gather.8.cloned.1.call-start
  502.3 0.1 dynamic_slice.24
  502.4 41.0 %all-reduce.5.cloned.1.call-done = (f32[128,256]{1,0:T(8,128)}, f32[128,256]{1,0:T(8,128)}) async-done(((f32[128,256]{1,0:T(8,128)}, f32[128,256]{1,0:T(8,128)}), (f32[128,256]{1,0:T(8,128)}, f32[128,256]{1,0:T(8,128)})) %all-reduce.5.cloned.1.call-update) | async-done | bytes 262160 | tf_op jit(solution)/shard_map/psum | solution.py:56
  543.4 1.0 broadcast_multiply_fusion
  544.4 0.1 copy.38
  544.5 0.1 copy.40
  544.6 2.9 fusion.26
  547.5 2.9 copy.41
  550.4 0.0 all-gather.8.cloned.1.call-update
  550.4 0.0 copy-start.7
  550.4 87.6 %all-gather.8.cloned.1.call-done = bf16[128,128,256]{2,0,1:T(8,128)(2,1)} async-done(((bf16[128,32,256]{2,0,1:T(8,128)(2,1)}), bf16[128,128,256]{2,0,1:T(8,128)(2,1)}) %all-gather.8.cloned.1.call-update) | async-done | bytes 8388624 | tf_op jit(solution)/shard_map/all_gather | solution.py:64
  638.0 0.0 copy-done
  638.0 8.7 %fusion = f32[32,128,256]{2,0,1:T(8,128)S(1)} fusion(bf16[128,128,256]{2,0,1:T(8,128)(2,1)} %all-gather.8.cloned.1.call-done, bf16[128,128]{1,0:T(8,128)(2,1)S(1)} %copy-done, s32[]{:T(128)S(6)} %select_n.20), kind=kOutput, calls=%fused_computation | convolution fusion | flops 268435456 | bytes 12615684 | tf_op jit(solution)/shard_map/hc,ihj->cij/dot_general | solution.py:66
  646.7 5.2 multiply_convert_fusion
  651.9 2.5 copy.43
  (11 shorter events, 0.1 us)
Async XLA Ops:
  6.5 631.5 %copy-start = (bf16[128,128]{1,0:T(8,128)(2,1)S(1)}, bf16[128,128]{1,0:T(8,128)(2,1)}, u32[]{:S(2)}) copy-start(bf16[128,128]{1,0:T(8,128)(2,1)} %param.13) | copy-start | bytes 98308
  6.5 51.8 %copy-start.1 = (bf16[32,128,256]{2,1,0:T(8,128)(2,1)S(1)}, bf16[32,128,256]{2,1,0:T(8,128)(2,1)}, u32[]{:S(2)}) copy-start(bf16[32,128,256]{2,1,0:T(8,128)(2,1)} %param.7) | copy-start | bytes 6291460
  6.5 149.7 %copy-start.5 = (bf16[4,128,128]{2,1,0:T(8,128)(2,1)S(1)}, bf16[4,128,128]{2,1,0:T(8,128)(2,1)}, u32[]{:S(2)}) copy-start(bf16[4,128,128]{2,1,0:T(8,128)(2,1)} %param.10) | copy-start | bytes 393220
  6.5 150.2 %copy-start.6 = (s32[128,256]{1,0:T(8,128)S(1)}, s32[128,256]{1,0:T(8,128)}, u32[]{:S(2)}) copy-start(s32[128,256]{1,0:T(8,128)} %param.8) | copy-start | bytes 393220
  6.5 50.8 %all-reduce.7.cloned.1.call-start = ((), (), s32[]{:S(2)}) async-start(), calls=%async_computation.5 | async-start | bytes 524288 | tf_op jit(solution)/shard_map/psum | solution.py:27
  11.4 229.6 %all-gather.6.cloned.1.call-start = ((), (), s32[]{:S(2)}) async-start(), calls=%async_computation.2 | async-start | bytes 6291456 | tf_op jit(solution)/shard_map/all_gather | solution.py:47
  60.0 47.8 %collective-permute-start = (bf16[32,128,256]{2,0,1:T(8,128)(2,1)S(1)}, bf16[32,128,256]{2,0,1:T(8,128)(2,1)S(1)}, u32[]{:S(2)}, u32[]{:S(2)}) collective-permute-start(bf16[32,128,256]{2,0,1:T(8,128)(2,1)S(1)} %fusion.12), channel_id=1, source_target_pairs={{0,1},{1,2},{2,3},{3,0},{4,5},{5,6},{6,7},{7,4},{8,9},{9,10},{10,1... | collective-permute-start | bytes 6291464 | tf_op jit(solution)/shard_map/ppermute | solution.py:36
  107.9 1.3 copy-start.3
  109.2 47.0 %collective-permute-start.1 = (bf16[32,128,256]{2,0,1:T(8,128)(2,1)S(1)}, bf16[32,128,256]{2,0,1:T(8,128)(2,1)}, u32[]{:S(2)}, u32[]{:S(2)}) collective-permute-start(bf16[32,128,256]{2,0,1:T(8,128)(2,1)S(1)} %collective-permute-done), channel_id=1, source_target_pairs={{0,1},{1,2},{2,3},{3,0},{4,5},{5,6},{6,7},{7,4},{8,9},{9,10},{10,1... | collective-permute-start | bytes 6291464 | tf_op jit(solution)/shard_map/ppermute | solution.py:36
  156.2 46.4 %collective-permute-start.2 = (bf16[32,128,256]{2,0,1:T(8,128)(2,1)}, bf16[32,128,256]{2,0,1:T(8,128)(2,1)}, u32[]{:S(2)}, u32[]{:S(2)}) collective-permute-start(bf16[32,128,256]{2,0,1:T(8,128)(2,1)} %collective-permute-done.1), channel_id=1, source_target_pairs={{0,1},{1,2},{2,3},{3,0},{4,5},{5,6},{6,7},{7,4},{8,9},{9,10},{10,1... | collective-permute-start | bytes 6291464 | tf_op jit(solution)/shard_map/ppermute | solution.py:36
  156.8 49.4 %copy-start.4 = (bf16[32,128,256]{2,0,1:T(8,128)(2,1)S(1)}, bf16[32,128,256]{2,0,1:T(8,128)(2,1)}, u32[]{:S(2)}) copy-start(bf16[32,128,256]{2,0,1:T(8,128)(2,1)} %copy-done.3) | copy-start | bytes 6291460
  213.5 5.7 copy-start.2
  228.3 254.6 %all-gather.4.cloned.1.call-start = ((), (), s32[]{:S(2)}) async-start(), calls=%async_computation.1 | async-start | bytes 10485760 | tf_op jit(solution)/shard_map/all_gather | solution.py:52
  229.0 314.3 %all-reduce.5.cloned.1.call-start = ((), (), s32[]{:S(2)}) async-start(), calls=%async_computation.4 | async-start | bytes 524288 | tf_op jit(solution)/shard_map/psum | solution.py:56
  482.9 19.4 %copy-start.8 = (f32[128]{0:T(128)S(1)}, f32[128]{0:T(128)}, u32[]{:S(2)}) copy-start(f32[128]{0:T(128)} %param.12) | copy-start | bytes 1540
  502.0 136.0 %all-gather.8.cloned.1.call-start = ((), (), s32[]{:S(2)}) async-start(), calls=%async_computation.3 | async-start | bytes 10485760 | tf_op jit(solution)/shard_map/all_gather | solution.py:64
  550.4 96.3 %copy-start.7 = (bf16[128,128]{1,0:T(8,128)(2,1)S(1)}, bf16[128,128]{1,0:T(8,128)(2,1)}, u32[]{:S(2)}) copy-start(bf16[128,128]{1,0:T(8,128)(2,1)} %param.11) | copy-start | bytes 98308
Sparse Core Ops, SparseCore 0:
  11.5 45.8 all-reduce.6
  228.4 12.5 all-gather.5
  242.6 240.2 all-gather.3
  502.1 41.2 all-reduce.4
  550.5 87.4 all-gather.7
